TPU v7x, 32 devices: a whole 2x2x4 slice. The times are simulated.
32 devices in a mesh: band: 16 (over z, x, core), ga: 2 (over y).
Axes of the slice: x: 2, y: 2, z: 4, core: 2. Of those that a mesh axis runs over, the one named last changes fastest.
Arguments:
- psi: float32 [2, 4096, 65536], P(None, 'band', 'ga'), may hold values from -0.0234375 to 0.0234375
- hx: float32 [2, 256, 65536], P(None, 'band', 'ga'), may hold values from -6 to 6
Outputs:
- h_sub: float32 [2, 4096, 256], P(None, ('band', 'ga'))
All inputs are finite; a program needn't handle non-finite values.
Results may differ from a plain program's by a relative error of at most 0.00007.
Values sent between devices are 32-bit elements; how exact they have to be, the bound alone decides.
A program may use at most 192 MiB of HBM per device.

v0:
```python
import jax
import jax.numpy as jnp
from jax import lax
from jax.sharding import PartitionSpec as P


def contract(left, right):
    return lax.dot_general(
        left,
        right,
        (((1,), (1,)), ((), ())),
        precision=lax.Precision.HIGHEST,
        preferred_element_type=jnp.float32,
    )


def per_device(psi, hx):
    psi_real = psi[0]
    psi_imag = psi[1]
    psi_diff = psi_real - psi_imag
    piece = lax.all_gather(hx, "band", axis=1, tiled=True)
    first = contract(psi_real, piece[0])
    second = contract(psi_imag, piece[1])
    third = contract(psi_diff, piece[0] + piece[1])
    partial_value = jnp.stack([first + second, third - first + second], axis=0)
    return lax.psum_scatter(partial_value, "ga", scatter_dimension=1, tiled=True)


def solution(mesh):
    in_specs = (P(None, "band", "ga"), P(None, "band", "ga"))
    out_specs = P(None, ("band", "ga"), None)
    return jax.shard_map(
        per_device, mesh=mesh, in_specs=in_specs, out_specs=out_specs, check_vma=False
    )
```

profile of v0, /device:TPU:0, one launch (start us, length us, event | category | flops | bytes accessed | tf_op | source)
XLA Modules:
  0.0 470.2 jit_solution(1202767534108503046)
XLA Ops:
  6.5 0.0 all-gather.2.cloned.1.call-start
  6.5 0.7 all-gather.2.cloned.1.call-update
  7.3 0.0 reduce-scatter.2.cloned.1.call-start
  7.3 330.4 %all-gather.2.cloned.1.call-done = f32[2,256,32768]{2,1,0:T(8,128)} async-done(((f32[2,16,32768]{2,1,0:T(8,128)}), f32[2,256,32768]{2,1,0:T(8,128)}) %all-gather.2.cloned.1.call-update) | async-done | bytes 67108880 | tf_op jit(solution)/shard_map/all_gather | solution.py:21
  337.7 32.9 %fusion.3 = f32[256,256]{1,0:T(8,128)S(1)} fusion(f32[2,256,32768]{2,1,0:T(8,128)} %all-gather.2.cloned.1.call-done, f32[2,256,32768]{2,1,0:T(8,128)} %param.2), kind=kOutput, calls=%fused_computation.3 | convolution fusion | flops 25769803776 | bytes 67371008 | tf_op jit(solution)/shard_map/dot_general | solution.py:8
  370.6 32.9 %fusion.6 = f32[256,256]{1,0:T(8,128)S(1)} fusion(f32[2,256,32768]{2,1,0:T(8,128)} %all-gather.2.cloned.1.call-done, f32[2,256,32768]{2,1,0:T(8,128)} %param.2), kind=kOutput, calls=%fused_computation.6 | convolution fusion | flops 25769803776 | bytes 67371008 | tf_op jit(solution)/shard_map/dot_general | solution.py:8
  403.6 44.2 %fusion.29 = f32[1,256,256]{2,1,0:T(8,128)S(1)} fusion(f32[256,256]{1,0:T(8,128)S(1)} %fusion.3, f32[256,256]{1,0:T(8,128)S(1)} %fusion.6, f32[2,256,32768]{2,1,0:T(8,128)} %all-gather.2.cloned.1.call-done, f32[2,256,32768]{2,1,0:T(8,128)} %param.2), kind=kOutput, calls=%fused_computation.21 | convolution fusion | flops 25786712064 | bytes 135004160 | tf_op jit(solution)/shard_map/dot_general | solution.py:8
  447.8 0.8 pad_maximum_fusion
  448.6 0.0 reduce-scatter.2.cloned.1.call-update
  448.6 14.8 %reduce-scatter.2.cloned.1.call-done = f32[2,128,256]{2,1,0:T(8,128)} async-done(((f32[2,256,256]{2,1,0:T(8,128)}), f32[2,128,256]{2,1,0:T(8,128)}) %reduce-scatter.2.cloned.1.call-update) | async-done | bytes 262160 | tf_op jit(solution)/shard_map/reduce_scatter | solution.py:26
  (1 shorter events, 0.0 us)
Async XLA Ops:
  6.5 331.2 %all-gather.2.cloned.1.call-start = ((), (), s32[]{:S(2)}) async-start(), calls=%async_computation.1 | async-start | bytes 71303168 | tf_op jit(solution)/shard_map/all_gather | solution.py:21
  7.3 456.1 %reduce-scatter.2.cloned.1.call-start = ((), (), s32[]{:S(2)}) async-start(), calls=%async_computation.2 | async-start | bytes 786432 | tf_op jit(solution)/shard_map/reduce_scatter | solution.py:26
Sparse Core Ops, SparseCore 0:
  8.9 328.7 all-gather.1
  448.7 14.6 reduce-scatter.1
where the time goes:
time: 470 us
  waiting for transfers between devices  346 us (74%)
  matrix products  110 us (23%)
  between operations  13.4 us (3%)
    all_gather x1, waiting for transfers between devices, per_device(): piece = lax.all_gather(hx, 'band', axis=1, tiled=True)  330 us
    dot_general x3, matrix products, contract(): lax.dot_general(left, right, (((1,), (1,)), ((), ())), precision=lax.Prec...  110 us
    reduce_scatter x1, waiting for transfers between devices, per_device(): lax.psum_scatter(partial_value, 'ga', scatter_dimension=1, tiled=True)  14.8 us
  transfers between devices with their start and end apart: 2, of which 2 were waited for; matrix products, arithmetic and copies ran while one was open for 0% of the time, Pallas kernels for 0%

commit v1 on v0

v1 whole, which is shorter than its diff:
```python
import jax
import jax.numpy as jnp
from jax import lax
from jax.sharding import PartitionSpec as P

SHARES = (22, 10)


def contract(left, right):
    return lax.dot_general(
        left,
        right,
        (((1,), (1,)), ((), ())),
        precision=lax.Precision.HIGH,
        preferred_element_type=jnp.float32,
    )


def per_device(psi, hx):
    parts, rows, depth = psi.shape
    unit = depth // sum(SHARES)
    bands = psi.reshape(parts * rows, depth)
    total = None
    first = 0
    pieces = []
    for share in SHARES:
        last = first + share * unit
        piece = lax.all_gather(hx[:, :, first:last], "band", axis=1, tiled=True)
        pieces.append((first, last, piece))
        first = last
    for first, last, piece in pieces:
        product = contract(bands[:, first:last], piece.reshape(-1, last - first))
        total = product if total is None else total + product
    vectors = total.shape[1] // parts
    real_left, imag_left = total[:rows], total[rows:]
    real_tile = real_left[:, :vectors] + imag_left[:, vectors:]
    imag_tile = real_left[:, vectors:] - imag_left[:, :vectors]
    partial_value = jnp.stack([real_tile, imag_tile], axis=0)
    n = lax.axis_size("ga")
    me = lax.axis_index("ga")
    height = rows // n

    def block(owner):
        return lax.dynamic_slice_in_dim(partial_value, owner * height, height, axis=1)

    result = block(me)
    for step in range(1, n):
        ring = [(i, (i + step) % n) for i in range(n)]
        result = result + lax.ppermute(block(lax.rem(me + step, n)), "ga", ring)
    return result


def solution(mesh):
    in_specs = (P(None, "band", "ga"), P(None, "band", "ga"))
    out_specs = P(None, ("band", "ga"), None)
    return jax.shard_map(
        per_device, mesh=mesh, in_specs=in_specs, out_specs=out_specs, check_vma=False
    )
```

time: 470 us -> 390 us (0.83)
  waiting for transfers between devices: 346 us -> 302 us
  matrix products: 110 us -> 66.2 us
  local copies, waits for them, and re-layouts: 0 us -> 6.08 us
    dot_general x3 -> x2, matrix products: 110 us -> 66.2 us  [contract(): lax.dot_general(left, right, (((1,), (1,)), ((), ())), precision=lax.Prec...]
    all_gather x1 -> x2, waiting for transfers between devices: 330 us -> 295 us  [per_device(): piece = lax.all_gather(hx[:, :, first:last], 'band', axis=1, tiled=True)]
    reduce_scatter x1 -> x0, waiting for transfers between devices: 14.8 us -> none  [per_device(): lax.psum_scatter(partial_value, 'ga', scatter_dimension=1, tiled=True)]
    ppermute x0 -> x1, waiting for transfers between devices: none -> 6.99 us  [per_device(): result = result + lax.ppermute(block(lax.rem(me + step, n)), 'ga', ring)]
    slice x0 -> x2, local copies, waits for them, and re-layouts: none -> 6.08 us  [per_device(): piece = lax.all_gather(hx[:, :, first:last], 'band', axis=1, tiled=True)]
  transfers between devices with their start and end apart: 2 -> 3, of which waited for: 2 -> 3; matrix products, arithmetic and copies ran while one was open for 0% -> 12% of each run, Pallas kernels for 0% -> 0%
where the time goes in v1:
time: 390 us
  waiting for transfers between devices  302 us (77%)
  matrix products  66.2 us (17%)
  between operations  13.4 us (3%)
  local copies, waits for them, and re-layouts  6.08 us (2%)
    all_gather x2, waiting for transfers between devices, per_device(): piece = lax.all_gather(hx[:, :, first:last], 'band', axis=1, tiled=True)  295 us
    dot_general x2, matrix products, contract(): lax.dot_general(left, right, (((1,), (1,)), ((), ())), precision=lax.Prec...  66.2 us
  transfers between devices with their start and end apart: 3, of which 3 were waited for; matrix products, arithmetic and copies ran while one was open for 12% of the time, Pallas kernels for 0%

profile of v1, /device:TPU:0, one launch (start us, length us, event | category | flops | bytes accessed | tf_op | source)
XLA Modules:
  0.0 389.9 jit_solution(5589482113664164910)
XLA Ops:
  6.5 0.0 all-gather.3.cloned.1.call-start
  6.5 3.6 slice.31
  10.1 0.0 all-gather.3.cloned.1.call-update
  10.2 0.0 all-gather.5.cloned.1.call-start
  10.2 2.5 slice.33
  12.7 0.0 all-gather.5.cloned.1.call-update
  12.7 227.6 %all-gather.3.cloned.1.call-done = f32[2,256,22528]{2,1,0:T(8,128)} async-done(((f32[2,16,22528]{2,1,0:T(8,128)}), f32[2,256,22528]{2,1,0:T(8,128)}) %all-gather.3.cloned.1.call-update) | async-done | bytes 46137360 | tf_op jit(solution)/shard_map/all_gather | solution.py:28
  240.3 43.3 %fusion = f32[512,512]{1,0:T(8,128)S(1)} fusion(f32[512,22528]{1,0:T(8,128)} %bitcast.9, f32[512,32768]{1,0:T(8,128)} %bitcast), kind=kOutput, calls=%fused_computation | convolution fusion | flops 35433480192 | bytes 93323264 | tf_op jit(solution)/shard_map/dot_general | solution.py:10
  283.6 67.1 %all-gather.5.cloned.1.call-done = f32[2,256,10240]{2,1,0:T(8,128)} async-done(((f32[2,16,10240]{2,1,0:T(8,128)}), f32[2,256,10240]{2,1,0:T(8,128)}) %all-gather.5.cloned.1.call-update) | async-done | bytes 20971536 | tf_op jit(solution)/shard_map/all_gather | solution.py:28
  350.7 22.9 %fusion.4 = f32[512,512]{1,0:T(8,128)S(1)} fusion(f32[512,512]{1,0:T(8,128)S(1)} %fusion, f32[512,10240]{1,0:T(8,128)} %bitcast.10, f32[512,32768]{1,0:T(8,128)} %bitcast), kind=kOutput, calls=%fused_computation.4 | convolution fusion | flops 16106389504 | bytes 44040192 | tf_op jit(solution)/shard_map/dot_general | solution.py:10
  373.6 0.1 fusion.10
  373.8 1.5 collective-permute-start
  375.3 7.0 %collective-permute-done = f32[2,128,256]{2,1,0:T(8,128)S(1)} collective-permute-done((f32[2,128,256]{2,1,0:T(8,128)S(1)}, f32[2,128,256]{2,1,0:T(8,128)S(1)}, u32[]{:S(2)}, u32[]{:S(2)}) %collective-permute-start) | collective-permute-done | bytes 262176 | tf_op jit(solution)/shard_map/ppermute | solution.py:49
  382.3 0.7 fusion.9
  (1 shorter events, 0.0 us)
Async XLA Ops:
  6.5 233.8 %all-gather.3.cloned.1.call-start = ((), (), s32[]{:S(2)}) async-start(), calls=%async_computation | async-start | bytes 49020928 | tf_op jit(solution)/shard_map/all_gather | solution.py:28
  10.2 340.5 %all-gather.5.cloned.1.call-start = ((), (), s32[]{:S(2)}) async-start(), calls=%async_computation.1 | async-start | bytes 22282240 | tf_op jit(solution)/shard_map/all_gather | solution.py:28
  373.8 8.5 %collective-permute-start = (f32[2,128,256]{2,1,0:T(8,128)S(1)}, f32[2,128,256]{2,1,0:T(8,128)S(1)}, u32[]{:S(2)}, u32[]{:S(2)}) collective-permute-start(f32[2,128,256]{2,1,0:T(8,128)S(1)} %fusion.7), channel_id=1, source_target_pairs={{0,1},{1,0},{2,3},{3,2},{4,5},{5,4},{6,7},{7,6},{8,9},{9,8},{10,11... | collective-permute-start | bytes 786440 | tf_op jit(solution)/shard_map/ppermute | solution.py:49
Sparse Core Ops, SparseCore 0:
  10.3 230.0 all-gather.2
  241.9 108.7 all-gather.4
